TPU v7x, 32 devices: a whole 2x2x4 slice. The times are simulated.
32 devices in a mesh: dp: 4 (over x, core), expert: 8 (over z, y).
Axes of the slice: x: 2, y: 2, z: 4, core: 2. Of those that a mesh axis runs over, the one named last changes fastest.
Arguments:
- tokens: bfloat16 [256, 7168], P('dp', 'expert'), parts along dimension 0, may hold values from -6 to 6
- routes: int32 [256, 8], P('dp'), parts along dimension 0, may hold values from 0 to 15, all different within a row; in each aligned block of 64 rows (0 to 63, 64 to 127, ...) at most 40 rows name the same one
- gate_values: bfloat16 [256, 8], P('dp'), parts along dimension 0, may hold values from 0.049804688 to 1
- gate_weight: bfloat16 [7168, 16384], P(None, 'expert'), may hold values from -0.0625 to 0.0625
- up_weight: bfloat16 [7168, 16384], P(None, 'expert'), may hold values from -0.0625 to 0.0625
- down_weight: bfloat16 [16384, 7168], P(None, 'expert'), may hold values from -0.1875 to 0.1875
Outputs:
- layer_output: bfloat16 [256, 7168], P('dp', 'expert'), parts along dimension 0
There are 4 independent parts, one for each index of `dp`. A program takes and returns all parts, laid end to end along the dimension named above; an argument that names none is the same for every part. Nothing has to cross between parts.
Inputs may be any that keep to these rules, and one draw needn't show every extreme that they name: `routes`: each row names 8 different experts; no expert is named by more than 40 rows of a group, a bound that some block reaches.
All inputs are finite; a program needn't handle non-finite values.
Results may differ from a plain program's by a relative error of at most 0.0049.
Values may be sent and summed in bfloat16 or wider, within the bound.
A program may use at most 128 MiB of HBM per device.

v0:
```python
import jax
import jax.numpy as jnp
from jax import lax
from jax.sharding import PartitionSpec as P

HIDDEN_SIZE = 1024
EXPERTS = 16


def body(tokens, routes, gate_values, gate_weight, up_weight, down_weight):
    unit_count = gate_weight.shape[1]
    span_units = min(unit_count, HIDDEN_SIZE)
    local_count = unit_count // span_units
    token_count = tokens.shape[0]
    first_expert = lax.axis_index("expert") * unit_count // HIDDEN_SIZE
    matched = routes[:, :, None] == lax.broadcasted_iota(jnp.int32, (1, 1, EXPERTS), 2)
    combine_table = jnp.sum(
        jnp.where(matched, gate_values[:, :, None].astype(jnp.float32), 0.0), axis=1
    )
    selector = (
        lax.broadcasted_iota(jnp.int32, (EXPERTS, local_count), 0)
        == first_expert + lax.broadcasted_iota(jnp.int32, (EXPERTS, local_count), 1)
    ).astype(jnp.float32)
    local_gates = jnp.dot(
        combine_table, selector, precision=lax.Precision.HIGHEST, preferred_element_type=jnp.float32
    )
    all_rows = lax.all_gather(tokens, "expert", axis=1, tiled=True)
    gate_proj = jnp.dot(all_rows, gate_weight, preferred_element_type=jnp.float32)
    up_proj = jnp.dot(all_rows, up_weight, preferred_element_type=jnp.float32)
    product = (jax.nn.silu(gate_proj) * up_proj).reshape(token_count, local_count, span_units)
    product = product * local_gates[:, :, None]
    hidden = product.reshape(token_count, unit_count).astype(jnp.bfloat16)
    result = jnp.dot(
        lax.all_gather(hidden, "expert", axis=1, tiled=True),
        down_weight,
        preferred_element_type=jnp.float32,
    )
    return result.astype(jnp.bfloat16)


def solution(mesh):
    in_specs = (
        P("dp", "expert"),
        P("dp", None),
        P("dp", None),
        P(None, "expert"),
        P(None, "expert"),
        P(None, "expert"),
    )
    out_specs = P("dp", "expert")
    return jax.shard_map(body, mesh=mesh, in_specs=in_specs, out_specs=out_specs, check_vma=False)
```

profile of v0, /device:TPU:0, one launch (start us, length us, event | category | flops | bytes accessed | tf_op | source)
XLA Modules:
  0.0 140.3 jit_solution(4098790935787080068)
XLA Ops:
  6.5 0.0 all-gather.2.cloned.1.call-start
  6.5 0.7 convert_element_type.11
  7.2 0.7 select_reduce_fusion
  7.9 0.2 fusion.2
  8.2 0.2 mul.24
  8.4 0.2 copy.12
  8.5 34.4 %all_gather.6 = bf16[64,7168]{1,0:T(8,128)(2,1)S(1)} all-gather(bf16[64,896]{1,0:T(8,128)(2,1)} %param.6), channel_id=1, replica_groups=mesh['dp'=4,'expert'=8] {'expert'}, dimensions={1}, use_global_device_ids=true | all-gather | bytes 1032192 | tf_op jit(solution)/shard_map/all_gather | solution.py:27
  42.9 12.1 %fusion.4 = f32[64,2048]{1,0:T(8,128)S(1)} fusion(bf16[64,7168]{1,0:T(8,128)(2,1)S(1)} %all_gather.6, bf16[7168,2048]{1,0:T(8,128)(2,1)} %param.9), kind=kOutput, calls=%fused_computation.10 | convolution fusion | flops 1879048192 | bytes 30801920 | tf_op jit(solution)/shard_map/dot_general | solution.py:28
  55.0 12.9 %fusion.1 = bf16[64,2048]{1,0:T(8,128)(2,1)} fusion(f32[64,2048]{1,0:T(8,128)S(1)} %bitcast.9, bf16[64,7168]{1,0:T(8,128)(2,1)S(1)} %all_gather.6, bf16[7168,2048]{1,0:T(8,128)(2,1)} %param.10, f32[64,2048]{1,0:T(8,128)S(1)} %fusion.4), kind=kOutput, calls=%fused_computation.2 | convolution fusion | flops 1879965696 | bytes 31588352 | tf_op jit(solution)/shard_map/dot_general | solution.py:29
  67.9 0.0 all-gather.2.cloned.1.call-update
  67.9 50.2 %all-gather.2.cloned.1.call-done = bf16[64,16384]{1,0:T(8,128)(2,1)} async-done(((bf16[64,2048]{1,0:T(8,128)(2,1)}), bf16[64,16384]{1,0:T(8,128)(2,1)}) %all-gather.2.cloned.1.call-update) | async-done | bytes 2097168 | tf_op jit(solution)/shard_map/all_gather | solution.py:34
  118.2 15.3 %convolution_convert_fusion = bf16[64,896]{1,0:T(8,128)(2,1)} fusion(bf16[64,16384]{1,0:T(8,128)(2,1)} %all-gather.2.cloned.1.call-done, bf16[16384,896]{1,0:T(8,128)(2,1)} %param.11), kind=kOutput, calls=%fused_computation.3 | convolution fusion | flops 1879105536 | bytes 31571968 | tf_op jit(solution)/shard_map/dot_general | solution.py:33
  (1 shorter events, 0.0 us)
Async XLA Ops:
  6.5 111.6 %all-gather.2.cloned.1.call-start = ((), (), s32[]{:S(2)}) async-start(), calls=%async_computation | async-start | bytes 2359296 | tf_op jit(solution)/shard_map/all_gather | solution.py:34
Sparse Core Ops, SparseCore 0:
  68.1 50.0 all-gather.1
where the time goes:
time: 140 us
  waiting for transfers between devices  50.3 us (36%)
  matrix products  40.5 us (29%)
  blocking collectives  34.4 us (25%)
  between operations  13.4 us (10%)
    all_gather x1, waiting for transfers between devices, body(): lax.all_gather(hidden, 'expert', axis=1, tiled=True)  50.2 us
    all_gather x1, blocking collectives, body(): all_rows = lax.all_gather(tokens, 'expert', axis=1, tiled=True)  34.4 us
    dot_general x1, matrix products, body(): jnp.dot(lax.all_gather(hidden, 'expert', axis=1, tiled=True), down_weight...  15.3 us
    dot_general x1, matrix products, body(): up_proj = jnp.dot(all_rows, up_weight, preferred_element_type=jnp.float32)  12.9 us
    dot_general x1, matrix products, body(): jnp.dot(all_rows, gate_weight, preferred_element_type=jnp.float32)  12.1 us
  transfers between devices with their start and end apart: 1, of which 1 were waited for; matrix products, arithmetic and copies ran while one was open for 0% of the time, Pallas kernels for 0%

commit v1 on v0

--- a/solution.py
+++ b/solution.py
@@ -31,7 +31,9 @@
     product = product * local_gates[:, :, None]
     hidden = product.reshape(token_count, unit_count).astype(jnp.bfloat16)
     result = jnp.dot(
-        lax.all_gather(hidden, "expert", axis=1, tiled=True),
+        jnp.concatenate(
+            lax.all_to_all(jnp.stack([hidden] * lax.axis_size("expert")), "expert", 0, 0), axis=1
+        ),
         down_weight,
         preferred_element_type=jnp.float32,
     )

time: 140 us -> 122 us (0.87)
  waiting for transfers between devices: 50.3 us -> 0 us
  blocking collectives: 34.4 us -> 82.3 us
  between operations: 13.4 us -> 0.05 us
  matrix products: 40.5 us -> 36.9 us
    all_gather x1 -> x0, waiting for transfers between devices: 50.2 us -> none  [body(): lax.all_gather(hidden, 'expert', axis=1, tiled=True)]
    all_to_all x0 -> x1, blocking collectives: none -> 47.9 us  [body(): lax.all_to_all(jnp.stack([hidden] * lax.axis_size('expert')), 'expert', 0...]
    dot_general x1, matrix products: 15.3 us -> 12.4 us  [body(): jnp.dot(jnp.concatenate(lax.all_to_all(jnp.stack([hidden] * lax.axis_size...]
  transfers between devices with their start and end apart: 1 -> 0, of which waited for: 1 -> 0; matrix products, arithmetic and copies ran while one was open for 0% -> 0% of each run, Pallas kernels for 0% -> 0%
where the time goes in v1:
time: 122 us; the launch traced here: 121 us
  blocking collectives  82.3 us (67%)
  matrix products  36.9 us (30%)
  other arithmetic  1.39 us (1%)
    all_to_all x1, blocking collectives, body(): lax.all_to_all(jnp.stack([hidden] * lax.axis_size('expert')), 'expert', 0...  47.9 us
    all_gather x1, blocking collectives, body(): all_rows = lax.all_gather(tokens, 'expert', axis=1, tiled=True)  34.4 us
    dot_general x1, matrix products, body(): jnp.dot(jnp.concatenate(lax.all_to_all(jnp.stack([hidden] * lax.axis_size...  12.4 us
    dot_general x1, matrix products, body(): up_proj = jnp.dot(all_rows, up_weight, preferred_element_type=jnp.float32)  12.2 us
    dot_general x1, matrix products, body(): jnp.dot(all_rows, gate_weight, preferred_element_type=jnp.float32)  12.1 us

profile of v1, /device:TPU:0, one launch (start us, length us, event | category | flops | bytes accessed | tf_op | source)
XLA Modules:
  0.0 121.4 jit_solution(4496944814511926825)
XLA Ops:
  0.0 0.7 convert_element_type.11
  0.7 0.7 select_reduce_fusion
  1.4 0.2 fusion.2
  1.6 0.2 mul.24
  1.8 0.2 copy.21
  2.0 34.4 %all_gather.3 = bf16[64,7168]{1,0:T(8,128)(2,1)S(1)} all-gather(bf16[64,896]{1,0:T(8,128)(2,1)} %param.6), channel_id=1, replica_groups=mesh['dp'=4,'expert'=8] {'expert'}, dimensions={1}, use_global_device_ids=true | all-gather | bytes 1032192 | tf_op jit(solution)/shard_map/all_gather | solution.py:27
  36.4 12.1 %fusion.4 = f32[64,2048]{1,0:T(8,128)S(1)} fusion(bf16[64,7168]{1,0:T(8,128)(2,1)S(1)} %all_gather.3, bf16[7168,2048]{1,0:T(8,128)(2,1)} %param.9), kind=kOutput, calls=%fused_computation.10 | convolution fusion | flops 1879048192 | bytes 30801920 | tf_op jit(solution)/shard_map/dot_general | solution.py:28
  48.4 12.2 %fusion.1 = bf16[64,2048]{1,0:T(8,128)(2,1)S(1)} fusion(f32[64,2048]{1,0:T(8,128)S(1)} %bitcast.14, bf16[64,7168]{1,0:T(8,128)(2,1)S(1)} %all_gather.3, bf16[7168,2048]{1,0:T(8,128)(2,1)} %param.10, f32[64,2048]{1,0:T(8,128)S(1)} %fusion.4), kind=kOutput, calls=%fused_computation.2 | convolution fusion | flops 1879965696 | bytes 31588352 | tf_op jit(solution)/shard_map/dot_general | solution.py:29
  60.7 0.2 stack.2
  60.9 47.9 %all_to_all.5 = bf16[8,64,2048]{2,1,0:T(8,128)(2,1)S(1)} all-to-all(bf16[8,64,2048]{2,1,0:T(8,128)(2,1)S(1)} %stack.2), channel_id=1, replica_groups=mesh['dp'=4,'expert'=8] {'expert'}, dimensions={0} | all-to-all | bytes 4194304 | tf_op jit(solution)/shard_map/all_to_all | solution.py:35
  108.8 0.1 copy.20
  108.9 12.4 %convolution_convert_fusion = bf16[64,896]{1,0:T(8,128)(2,1)} fusion(bf16[64,16384]{1,0:T(8,128)(2,1)S(1)} %bitcast.12, bf16[16384,896]{1,0:T(8,128)(2,1)} %param.11), kind=kOutput, calls=%fused_computation.3 | convolution fusion | flops 1879105536 | bytes 31571968 | tf_op jit(solution)/shard_map/dot_general | solution.py:33
  (1 shorter events, 0.0 us)
